TPU v7x, 32 devices: a whole 2x2x4 slice. The times are simulated.
32 devices in a mesh: ch: 16 (over z, x, core), rep: 2 (over y).
Axes of the slice: x: 2, y: 2, z: 4, core: 2. Of those that a mesh axis runs over, the one named last changes fastest.
Arguments:
- fields_a: bfloat16 [32, 128, 4096], P('rep', 'ch'), parts along dimension 0, may hold values from -6 to 6
- latent_b: bfloat16 [32, 2048, 512], P('rep', 'ch'), parts along dimension 0, may hold values from -6 to 6
- regrid_w: bfloat16 [32, 1, 128, 64], replicated, may hold values from -0.5 to 0.5
- cell_tiles: int32 [32, 1], replicated, may hold values from 0 to 31, as said below
- norm_a: float32 [128], replicated, may hold values from 0.5 to 1.5
- enc_in: bfloat16 [128, 512], replicated, may hold values from -0.5 to 0.5
- enc_mid: bfloat16 [512, 512], replicated, may hold values from -0.25 to 0.25
- enc_out: bfloat16 [512, 512], replicated, may hold values from -0.25 to 0.25
- norm_b: float32 [512], replicated, may hold values from 0.5 to 1.5
- dec_mid: bfloat16 [512, 512], replicated, may hold values from -0.25 to 0.25
- dec_out: bfloat16 [512, 128], replicated, may hold values from -0.25 to 0.25
Outputs:
- latent_a: bfloat16 [32, 2048, 512], P('rep', 'ch'), parts along dimension 0
- cells_b: bfloat16 [32, 128, 4096], P('rep', 'ch'), parts along dimension 0
There are 2 independent parts, one for each index of `rep`. A program takes and returns all parts, laid end to end along the dimension named above; an argument that names none is the same for every part. Nothing has to cross between parts.
Inputs may be any that keep to these rules, and one draw needn't show every extreme that they name: The one column of cell_tiles names every one of the 32 cell blocks exactly once.
All inputs are finite; a program needn't handle non-finite values.
Results may differ from a plain program's by a relative error of at most 0.0066.
Values may be sent and summed in bfloat16 or wider, within the bound.
A program may use at most 64 MiB of HBM per device.

v0:
```python
import jax
import jax.numpy as jnp
from jax import lax
from jax.sharding import PartitionSpec as P

BN = 64
BC = 128
K = 1
EPSILON = 1e-05


def normalize(values, gain_vec, along):
    average = jnp.mean(values, axis=along, keepdims=True)
    centred = values - average
    spread = jnp.mean(centred * centred, axis=along, keepdims=True)
    return centred * lax.rsqrt(spread + EPSILON) * gain_vec


def shards(
    fields_a,
    latent_b,
    regrid_w,
    cell_tiles,
    norm_a,
    enc_in,
    enc_mid,
    enc_out,
    norm_b,
    dec_mid,
    dec_out,
):
    groups = lax.axis_size("ch")
    samples = fields_a.shape[0]
    own_channels = fields_a.shape[1]
    blocks_all = cell_tiles.shape[0]
    node_rows = latent_b.shape[1]
    hidden = latent_b.shape[2]
    channels = own_channels * groups
    blocks = fields_a.reshape(samples, own_channels, blocks_all, BC)
    chosen = jnp.take(blocks, cell_tiles, axis=2).reshape(samples, own_channels, blocks_all, K * BC)
    weights = regrid_w.reshape(blocks_all, K * BC, BN)
    grid_vals = jnp.einsum("ecnj,njm->ecnm", chosen, weights, preferred_element_type=jnp.float32)
    grid_sent = grid_vals.astype(jnp.bfloat16).reshape(samples, own_channels, groups, node_rows)
    received_a = lax.all_to_all(grid_sent, "ch", split_axis=2, concat_axis=1, tiled=True)
    normed = normalize(latent_b.astype(jnp.float32), norm_b, 2).astype(jnp.bfloat16)
    middle = jax.nn.silu(
        jnp.einsum("enh,hg->eng", normed, dec_mid, preferred_element_type=jnp.float32)
    ).astype(jnp.bfloat16)
    out_split = dec_out.reshape(hidden, groups, own_channels)
    decoded_sent = jnp.einsum(
        "enh,hjc->ecjn", middle, out_split, preferred_element_type=jnp.float32
    ).astype(jnp.bfloat16)
    values = received_a.reshape(samples, channels, node_rows).astype(jnp.float32)
    normed = normalize(values, norm_a[:, None], 1).astype(jnp.bfloat16)
    base = jnp.einsum("ecn,ch->enh", normed, enc_in, preferred_element_type=jnp.float32).astype(
        jnp.bfloat16
    )
    middle = jax.nn.silu(
        jnp.einsum("enh,hg->eng", base, enc_mid, preferred_element_type=jnp.float32)
    ).astype(jnp.bfloat16)
    result = base.astype(jnp.float32) + jnp.einsum(
        "enh,hg->eng", middle, enc_out, preferred_element_type=jnp.float32
    )
    latent_a = result.astype(jnp.bfloat16)
    received_b = lax.all_to_all(decoded_sent, "ch", split_axis=2, concat_axis=1, tiled=True)
    arranged = received_b.reshape(samples, groups, own_channels, node_rows)
    node_blocks = jnp.moveaxis(arranged, 1, 2).reshape(samples, own_channels, blocks_all, BN)
    inverse = jnp.argsort(cell_tiles, axis=0).T
    picked = jnp.take(node_blocks, inverse, axis=2)
    weight_sel = regrid_w[inverse, jnp.arange(K)[:, None]]
    total = jnp.einsum("ecknm,knbm->ecnb", picked, weight_sel, preferred_element_type=jnp.float32)
    cells_b = total.astype(jnp.bfloat16).reshape(samples, own_channels, blocks_all * BC)
    return (latent_a, cells_b)


def solution(mesh):
    placed = (
        P("rep", "ch", None),
        P("rep", "ch", None),
        P(),
        P(),
        P(),
        P(),
        P(),
        P(),
        P(),
        P(),
        P(),
    )
    return jax.shard_map(
        shards,
        mesh=mesh,
        in_specs=placed,
        out_specs=(P("rep", "ch", None), P("rep", "ch", None)),
        check_vma=False,
    )
```

profile of v0, /device:TPU:0, one launch (start us, length us, event | category | flops | bytes accessed | tf_op | source)
XLA Modules:
  0.0 64.0 jit_solution(9747075597492145657)
XLA Ops:
  0.6 0.0 copy-start
  0.6 0.0 copy-start.2
  0.7 0.8 %fusion.60 = s32[32]{0:T(128)S(1)} fusion(s32[32,1]{0,1:T(1,128)} %param.14), kind=kLoop, calls=%fused_computation.72 | loop fusion | flops 96 | bytes 256 | tf_op jit(solution)/shard_map/jit(_take)/broadcast_in_dim | solution.py:40
  1.4 0.7 %and_bitcast_fusion = pred[32]{0:T(512)(128)(4,1)S(1)} fusion(s32[32,1]{0,1:T(1,128)} %param.14), kind=kLoop, calls=%fused_computation.66 | loop fusion | flops 192 | bytes 160 | tf_op jit(solution)/shard_map/jit(_take)/reduce_and | solution.py:40
  2.1 0.0 copy-done
  2.1 0.9 %gather_fusion = bf16[32,16,8,128]{3,2,1,0:T(8,128)(2,1)S(1)} fusion(bf16[16,8,32,128]{3,1,2,0:T(8,128)(2,1)S(1)} %bitcast.101, s32[1024]{0:T(1024)S(1)} %pad_clamp_fusion.1), kind=kCustom, calls=%fused_computation | custom fusion | bytes 2097280 | tf_op jit(solution)/shard_map/jit(_take)/gather | solution.py:40
  3.1 0.0 copy-done.2
  3.1 0.5 fusion.14
  3.6 1.6 %copy.42 = bf16[16,8,32,64]{3,2,1,0:T(8,128)(2,1)} copy(bf16[16,8,32,64]{3,1,0,2:T(8,128)(2,1)S(1)} %fusion.14) | data formatting | bytes 1048576 | tf_op jit(solution)/shard_map/convert_element_type | solution.py:43
  5.2 2.6 %reshape.150 = bf16[16,8,16,128]{3,2,1,0:T(8,128)(2,1)} reshape(bf16[16,8,32,64]{3,2,1,0:T(8,128)(2,1)} %copy.42) | data formatting | bytes 1048576 | tf_op jit(solution)/shard_map/reshape | solution.py:43
  7.8 2.0 %copy.43 = bf16[16,8,16,128]{3,1,0,2:T(8,128)(2,1)} copy(bf16[16,8,16,128]{3,2,1,0:T(8,128)(2,1)} %reshape.150) | data formatting | bytes 1048576 | tf_op jit(solution)/shard_map/reshape | solution.py:43
  9.8 7.4 %all-to-all-start = ((bf16[16,8,16,128]{3,1,0,2:T(8,128)(2,1)}), bf16[16,8,16,128]{3,1,0,2:T(8,128)(2,1)}, u32[]{:S(2)}, u32[]{:S(2)}) async-start(bf16[16,8,16,128]{3,1,0,2:T(8,128)(2,1)} %copy.43), calls=%async_computation | async-start | bytes 1048576 | tf_op jit(solution)/shard_map/all_to_all | solution.py:44
  17.2 0.0 copy-done.1
  17.2 0.0 copy-start.5
  17.2 0.0 copy-start.8
  17.2 0.3 convert_reduce_fusion
  17.6 1.0 %fusion.2 = f32[16,128]{1,0:T(8,128)S(1)} fusion(bf16[16,128,512]{2,1,0:T(8,128)(2,1)S(1)} %copy-done.1, f32[16,128]{1,0:T(8,128)S(1)} %broadcast_multiply_fusion), kind=kLoop, calls=%fused_computation.7 | loop fusion | flops 4192256 | bytes 2113536 | tf_op jit(solution)/shard_map/reduce_sum | solution.py:15
  18.6 0.0 copy-done.5
  18.6 0.1 copy.47
  18.7 0.0 copy-done.8
  18.7 0.0 copy-start.7
  18.8 4.4 %fusion.25 = bf16[16,8,16,128]{3,2,1,0:T(8,128)(2,1)} fusion(bf16[16,128,512]{2,1,0:T(8,128)(2,1)S(1)} %copy-done.1, f32[512]{0:T(512)S(1)} %copy-done.8, f32[16,128]{1,0:T(8,128)S(1)} %add_rsqrt_fusion, f32[16,128]{1,0:T(8,128)S(1)} %broadcast_multiply_fusion, bf16[512,512]{1,0:T(8,128)(2,1)} %param.20, bf16[512,16,8]{0,2,1:T(8,128)(2,1)S(1)} %bitcast.102), kind=kOutput, calls=%fused_computation.30 | convolution fusion | flops 1352925184 | bytes 3295232 | tf_op jit(solution)/shard_map/enh,hjc->ecjn/dot_general | solution.py:50
  23.1 0.0 copy-done.7
  23.1 0.1 copy.46
  23.2 2.0 %copy.49 = bf16[16,8,16,128]{3,1,0,2:T(8,128)(2,1)} copy(bf16[16,8,16,128]{3,2,1,0:T(8,128)(2,1)} %fusion.25) | data formatting | bytes 1048576 | tf_op jit(solution)/shard_map/convert_element_type | solution.py:52
  25.3 0.8 %sort.17 = (s32[32,1]{1,0:T(8,128)}, s32[32,1]{1,0:T(8,128)S(1)}) sort(s32[32,1]{1,0:T(8,128)S(1)} %copy.46, s32[32,1]{1,0:T(8,128)S(1)} %iota.7), dimensions={0}, to_apply=%region_2.3 | sort | flops 160 | bytes 512 | tf_op jit(solution)/shard_map/jit(argsort)/sort | solution.py:68
  26.1 0.1 reduce.2
  26.2 5.3 %all-to-all-done = bf16[16,8,16,128]{3,1,0,2:T(8,128)(2,1)} async-done(((bf16[16,8,16,128]{3,1,0,2:T(8,128)(2,1)}), bf16[16,8,16,128]{3,1,0,2:T(8,128)(2,1)}, u32[]{:S(2)}, u32[]{:S(2)}) %all-to-all-start) | async-done | bytes 524320 | tf_op jit(solution)/shard_map/all_to_all | solution.py:44
  31.5 4.2 %all-to-all-start.1 = ((bf16[16,8,16,128]{3,1,0,2:T(8,128)(2,1)}), bf16[16,8,16,128]{3,1,0,2:T(8,128)(2,1)S(1)}, u32[]{:S(2)}, u32[]{:S(2)}) async-start(bf16[16,8,16,128]{3,1,0,2:T(8,128)(2,1)} %copy.49), calls=%async_computation.1 | async-start | bytes 1048576 | tf_op jit(solution)/shard_map/all_to_all | solution.py:65
  35.7 0.0 copy-done.3
  35.7 0.6 %gather_fusion.1 = bf16[32,128,64]{1,2,0:T(8,128)(2,1)S(1)} fusion(bf16[32,1,128,64]{2,3,1,0:T(8,128)(2,1)S(1)} %copy-done.3, s32[32]{0:T(128)S(1)} %or_bitcast_fusion), kind=kCustom, calls=%fused_computation.1 | custom fusion | bytes 1048832 | tf_op jit(solution)/shard_map/gather | solution.py:70
  36.4 1.1 %fusion.16 = f32[16,128]{1,0:T(8,128)S(1)} fusion(bf16[16,8,16,128]{3,1,0,2:T(8,128)(2,1)} %all-to-all-done), kind=kLoop, calls=%fused_computation.27 | loop fusion | flops 522240 | bytes 532480 | tf_op jit(solution)/shard_map/reduce_sum | solution.py:13
  37.6 1.2 %fusion.31 = f32[16,128]{1,0:T(8,128)S(1)} fusion(f32[16,128]{1,0:T(8,128)S(1)} %broadcast_multiply_fusion.1, bf16[16,8,16,128]{3,1,0,2:T(8,128)(2,1)} %all-to-all-done), kind=kLoop, calls=%fused_computation.32 | loop fusion | flops 1046528 | bytes 540672 | tf_op jit(solution)/shard_map/reduce_sum | solution.py:15
  38.8 11.2 %all-to-all-done.1 = bf16[16,8,16,128]{3,1,0,2:T(8,128)(2,1)S(1)} async-done(((bf16[16,8,16,128]{3,1,0,2:T(8,128)(2,1)}), bf16[16,8,16,128]{3,1,0,2:T(8,128)(2,1)S(1)}, u32[]{:S(2)}, u32[]{:S(2)}) %all-to-all-start.1) | async-done | bytes 524320 | tf_op jit(solution)/shard_map/all_to_all | solution.py:65
  50.0 0.3 copy.50
  50.3 0.4 reshape.153
  50.7 1.4 %copy.51 = bf16[16,8,32,64]{3,1,2,0:T(8,128)(2,1)} copy(bf16[16,8,32,64]{3,2,1,0:T(8,128)(2,1)S(1)} %reshape.153) | data formatting | bytes 1048576 | tf_op jit(solution)/shard_map/reshape | solution.py:67
  52.1 2.2 %gather_fusion.2 = bf16[32,16,8,64]{3,2,1,0:T(8,128)(2,1)S(1)} fusion(bf16[16,8,32,64]{3,1,2,0:T(8,128)(2,1)} %copy.51, s32[1024]{0:T(1024)S(1)} %pad_clamp_fusion), kind=kCustom, calls=%fused_computation.2 | custom fusion | bytes 1048704 | tf_op jit(solution)/shard_map/jit(_take)/gather | solution.py:69
  54.3 0.2 select_bitcast_fusion
  54.5 0.4 fusion.15
  54.9 0.0 copy-start.4
  54.9 0.0 copy-start.6
  54.9 0.7 %copy.53 = bf16[16,8,32,128]{3,2,1,0:T(8,128)(2,1)S(1)} copy(bf16[16,8,32,128]{3,0,1,2:T(8,128)(2,1)S(1)} %fusion.15) | data formatting | bytes 2097152 | tf_op jit(solution)/shard_map/convert_element_type | solution.py:72
  55.6 1.3 %reshape.154 = bf16[16,8,4096]{2,1,0:T(8,128)(2,1)} reshape(bf16[16,8,32,128]{3,2,1,0:T(8,128)(2,1)S(1)} %copy.53) | data formatting | bytes 2097152 | tf_op jit(solution)/shard_map/reshape | solution.py:72
  56.9 0.0 copy-done.4
  56.9 0.0 copy-done.6
  56.9 1.8 %convolution_convert_fusion = bf16[16,128,512]{2,1,0:T(8,128)(2,1)S(1)} fusion(f32[128]{0:T(128)S(1)} %copy-done.6, f32[16,128]{1,0:T(8,128)S(1)} %add_rsqrt_fusion.1, f32[16,128]{1,0:T(8,128)S(1)} %broadcast_multiply_fusion.1, bf16[16,8,16,128]{3,1,0,2:T(8,128)(2,1)} %all-to-all-done, bf16[128,512]{1,0:T(8,128)(2,1)S(1)} %copy-done.4), kind=kOutput, calls=%fused_computation.19 | convolution fusion | flops 270794752 | bytes 2769408 | tf_op jit(solution)/shard_map/ecn,ch->enh/dot_general | solution.py:55
  58.8 5.2 %add_convert_fusion = bf16[16,128,512]{2,1,0:T(8,128)(2,1)} fusion(bf16[16,128,512]{2,1,0:T(8,128)(2,1)S(1)} %convolution_convert_fusion, bf16[512,512]{1,0:T(8,128)(2,1)} %param.18, bf16[512,512]{1,0:T(8,128)(2,1)} %param.17), kind=kOutput, calls=%fused_computation.11 | convolution fusion | flops 2155872256 | bytes 5242880 | tf_op jit(solution)/shard_map/enh,hg->eng/dot_general | solution.py:61
  (13 shorter events, 0.1 us)
Async XLA Ops:
  0.6 1.5 %copy-start = (bf16[16,8,4096]{2,1,0:T(8,128)(2,1)S(1)}, bf16[16,8,4096]{2,1,0:T(8,128)(2,1)}, u32[]{:S(2)}) copy-start(bf16[16,8,4096]{2,1,0:T(8,128)(2,1)} %param.11) | copy-start | bytes 3145732
  0.6 2.4 %copy-start.2 = (bf16[32,1,128,64]{2,3,1,0:T(8,128)(2,1)S(1)}, bf16[32,1,128,64]{2,3,1,0:T(8,128)(2,1)}, u32[]{:S(2)}) copy-start(bf16[32,1,128,64]{2,3,1,0:T(8,128)(2,1)} %param.13) | copy-start | bytes 1572868
  5.2 12.0 %copy-start.1 = (bf16[16,128,512]{2,1,0:T(8,128)(2,1)S(1)}, bf16[16,128,512]{2,1,0:T(8,128)(2,1)}, u32[]{:S(2)}) copy-start(bf16[16,128,512]{2,1,0:T(8,128)(2,1)} %param.12) | copy-start | bytes 6291460
  9.8 21.8 %all-to-all-start = ((bf16[16,8,16,128]{3,1,0,2:T(8,128)(2,1)}), bf16[16,8,16,128]{3,1,0,2:T(8,128)(2,1)}, u32[]{:S(2)}, u32[]{:S(2)}) async-start(bf16[16,8,16,128]{3,1,0,2:T(8,128)(2,1)} %copy.43), calls=%async_computation | async-start | bytes 1048576 | tf_op jit(solution)/shard_map/all_to_all | solution.py:44
  17.2 1.4 %copy-start.5 = (bf16[512,128]{1,0:T(8,128)(2,1)S(1)}, bf16[512,128]{1,0:T(8,128)(2,1)}, u32[]{:S(2)}) copy-start(bf16[512,128]{1,0:T(8,128)(2,1)} %param.21) | copy-start | bytes 393220
  17.2 1.5 %copy-start.8 = (f32[512]{0:T(512)S(1)}, f32[512]{0:T(512)}, u32[]{:S(2)}) copy-start(f32[512]{0:T(512)} %param.19) | copy-start | bytes 6148
  18.7 4.4 %copy-start.7 = (s32[32,1]{0,1:T(1,128)S(1)}, s32[32,1]{0,1:T(1,128)}, u32[]{:S(2)}) copy-start(s32[32,1]{0,1:T(1,128)} %param.14) | copy-start | bytes 388
  23.1 12.6 %copy-start.3 = (bf16[32,1,128,64]{2,3,1,0:T(8,128)(2,1)S(1)}, bf16[32,1,128,64]{2,3,1,0:T(8,128)(2,1)}, u32[]{:S(2)}) copy-start(bf16[32,1,128,64]{2,3,1,0:T(8,128)(2,1)} %param.13) | copy-start | bytes 1572868
  31.5 18.4 %all-to-all-start.1 = ((bf16[16,8,16,128]{3,1,0,2:T(8,128)(2,1)}), bf16[16,8,16,128]{3,1,0,2:T(8,128)(2,1)S(1)}, u32[]{:S(2)}, u32[]{:S(2)}) async-start(bf16[16,8,16,128]{3,1,0,2:T(8,128)(2,1)} %copy.49), calls=%async_computation.1 | async-start | bytes 1048576 | tf_op jit(solution)/shard_map/all_to_all | solution.py:65
  54.9 2.0 %copy-start.4 = (bf16[128,512]{1,0:T(8,128)(2,1)S(1)}, bf16[128,512]{1,0:T(8,128)(2,1)}, u32[]{:S(2)}) copy-start(bf16[128,512]{1,0:T(8,128)(2,1)} %param.16) | copy-start | bytes 393220
  54.9 2.0 %copy-start.6 = (f32[128]{0:T(128)S(1)}, f32[128]{0:T(128)}, u32[]{:S(2)}) copy-start(f32[128]{0:T(128)} %param.15) | copy-start | bytes 1540
where the time goes:
time: 64.6 us; the launch traced here: 64 us
  waiting for transfers between devices  16.5 us (26%)
  local copies, waits for them, and re-layouts  16.4 us (25%)
  matrix products  12.4 us (19%)
  starting transfers between devices  11.6 us (18%)
  other arithmetic  6.21 us (10%)
  between operations  0.9 us (1%)
    all_to_all x1, waiting for transfers between devices, shards(): lax.all_to_all(decoded_sent, 'ch', split_axis=2, concat_axis=1, tiled=True)  11.2 us
    all_to_all x1, starting transfers between devices, shards(): lax.all_to_all(grid_sent, 'ch', split_axis=2, concat_axis=1, tiled=True)  7.44 us
    all_to_all x1, waiting for transfers between devices, shards(): lax.all_to_all(grid_sent, 'ch', split_axis=2, concat_axis=1, tiled=True)  5.32 us
    dot_general x1, matrix products, shards(): jnp.einsum('enh,hg->eng', middle, enc_out, preferred_element_type=jnp.flo...  5.24 us
    reshape x2, local copies, waits for them, and re-layouts, shards(): grid_vals.astype(jnp.bfloat16)  4.55 us
    dot_general x1, matrix products, shards(): jnp.einsum('enh,hjc->ecjn', middle, out_split, preferred_element_type=jnp...  4.37 us
    all_to_all x1, starting transfers between devices, shards(): lax.all_to_all(decoded_sent, 'ch', split_axis=2, concat_axis=1, tiled=True)  4.17 us
    reduce_sum x2, other arithmetic, normalize(): spread = jnp.mean(centred * centred, axis=along, keepdims=True)  2.17 us
  transfers between devices with their start and end apart: 2, of which 2 were waited for; matrix products, arithmetic and copies ran while one was open for 19% of the time, Pallas kernels for 0%

commit v1 on v0

--- a/solution.py
+++ b/solution.py
@@ -62,7 +62,10 @@
         "enh,hg->eng", middle, enc_out, preferred_element_type=jnp.float32
     )
     latent_a = result.astype(jnp.bfloat16)
-    received_b = lax.all_to_all(decoded_sent, "ch", split_axis=2, concat_axis=1, tiled=True)
+    received_b = jnp.concatenate(
+        lax.all_to_all(jnp.stack(jnp.split(decoded_sent, lax.axis_size("ch"), axis=2)), "ch", 0, 0),
+        axis=1,
+    )
     arranged = received_b.reshape(samples, groups, own_channels, node_rows)
     node_blocks = jnp.moveaxis(arranged, 1, 2).reshape(samples, own_channels, blocks_all, BN)
     inverse = jnp.argsort(cell_tiles, axis=0).T

time: 64.6 us -> 74.1 us (1.15)
  local copies, waits for them, and re-layouts: 16.4 us -> 29.4 us
  waiting for transfers between devices: 16.5 us -> 11.2 us
  starting transfers between devices: 11.6 us -> 13.4 us
    unnamed x20 -> x33, local copies, waits for them, and re-layouts: 0.26 us -> 10.3 us
    all_to_all x1, waiting for transfers between devices: 5.32 us -> 0.01 us  [shards(): lax.all_to_all(grid_sent, 'ch', split_axis=2, concat_axis=1, tiled=True)]
    split x0 -> x1, local copies, waits for them, and re-layouts: none -> 4.4 us  [shards(): jnp.split(decoded_sent, lax.axis_size('ch'), axis=2)]
    convert_element_type x1 -> x0, local copies, waits for them, and re-layouts: 2.04 us -> none  [shards(): decoded_sent = jnp.einsum('enh,hjc->ecjn', middle, out_split, preferred_e...]
    all_to_all x1, starting transfers between devices: 4.17 us -> 5.96 us  [shards(): lax.all_to_all(jnp.stack(jnp.split(decoded_sent, lax.axis_size('ch'), axi...]
  transfers between devices with their start and end apart: 2 -> 2, of which waited for: 2 -> 1; matrix products, arithmetic and copies ran while one was open for 19% -> 32% of each run, Pallas kernels for 0% -> 0%
where the time goes in v1:
time: 74.1 us; the launch traced here: 73.4 us
  local copies, waits for them, and re-layouts  29.4 us (40%)
  starting transfers between devices  13.4 us (18%)
  matrix products  12.4 us (17%)
  waiting for transfers between devices  11.2 us (15%)
  other arithmetic  6.09 us (8%)
  between operations  0.9 us (1%)
    all_to_all x1, waiting for transfers between devices, shards(): lax.all_to_all(jnp.stack(jnp.split(decoded_sent, lax.axis_size('ch'), axi...  11.2 us
    unnamed x33, local copies, waits for them, and re-layouts  10.3 us
    all_to_all x1, starting transfers between devices, shards(): lax.all_to_all(grid_sent, 'ch', split_axis=2, concat_axis=1, tiled=True)  7.44 us
    all_to_all x1, starting transfers between devices, shards(): lax.all_to_all(jnp.stack(jnp.split(decoded_sent, lax.axis_size('ch'), axi...  5.96 us
    dot_general x1, matrix products, shards(): jnp.einsum('enh,hg->eng', middle, enc_out, preferred_element_type=jnp.flo...  5.25 us
    reshape x2, local copies, waits for them, and re-layouts, shards(): grid_vals.astype(jnp.bfloat16)  4.55 us
    split x1, local copies, waits for them, and re-layouts, shards(): jnp.split(decoded_sent, lax.axis_size('ch'), axis=2)  4.4 us
    dot_general x1, matrix products, shards(): jnp.einsum('enh,hjc->ecjn', middle, out_split, preferred_element_type=jnp...  4.37 us
  transfers between devices with their start and end apart: 2, of which 1 were waited for; matrix products, arithmetic and copies ran while one was open for 32% of the time, Pallas kernels for 0%

profile of v1, /device:TPU:0, one launch (start us, length us, event | category | flops | bytes accessed | tf_op | source)
XLA Modules:
  0.0 73.4 jit_solution(10340148514329407295)
XLA Ops:
  0.6 0.0 copy-start
  0.7 0.9 %copy.298 = s32[32,1]{1,0:T(8,128)S(1)} copy(s32[32,1]{0,1:T(1,128)} %param.14) | data formatting | bytes 256 | tf_op args[3]
  1.5 0.7 fusion.60
  2.2 0.7 and_bitcast_fusion
  2.8 0.8 %sort.17 = (s32[32,1]{1,0:T(8,128)}, s32[32,1]{1,0:T(8,128)S(1)}) sort(s32[32,1]{1,0:T(8,128)S(1)} %copy.298, s32[32,1]{1,0:T(8,128)S(1)} %iota.7), dimensions={0}, to_apply=%region_2.3 | sort | flops 160 | bytes 512 | tf_op jit(solution)/shard_map/jit(argsort)/sort | solution.py:71
  3.6 0.1 reduce.2
  3.8 0.9 %gather_fusion = bf16[32,16,8,128]{3,2,1,0:T(8,128)(2,1)S(1)} fusion(bf16[16,8,32,128]{3,1,2,0:T(8,128)(2,1)S(1)} %bitcast.138, s32[1024]{0:T(1024)S(1)} %get-tuple-element.23), kind=kCustom, calls=%fused_computation | custom fusion | bytes 2097280 | tf_op jit(solution)/shard_map/jit(_take)/gather | solution.py:40
  4.7 0.5 fusion.14
  5.2 1.6 %copy.294 = bf16[16,8,32,64]{3,2,1,0:T(8,128)(2,1)} copy(bf16[16,8,32,64]{3,1,0,2:T(8,128)(2,1)S(1)} %fusion.14) | data formatting | bytes 1048576 | tf_op jit(solution)/shard_map/convert_element_type | solution.py:43
  6.9 2.6 %reshape.151 = bf16[16,8,16,128]{3,2,1,0:T(8,128)(2,1)} reshape(bf16[16,8,32,64]{3,2,1,0:T(8,128)(2,1)} %copy.294) | data formatting | bytes 1048576 | tf_op jit(solution)/shard_map/reshape | solution.py:43
  9.5 2.0 %copy.295 = bf16[16,8,16,128]{3,1,0,2:T(8,128)(2,1)} copy(bf16[16,8,16,128]{3,2,1,0:T(8,128)(2,1)} %reshape.151) | data formatting | bytes 1048576 | tf_op jit(solution)/shard_map/reshape | solution.py:43
  11.4 7.4 %all-to-all-start = ((bf16[16,8,16,128]{3,1,0,2:T(8,128)(2,1)}), bf16[16,8,16,128]{3,1,0,2:T(8,128)(2,1)}, u32[]{:S(2)}, u32[]{:S(2)}) async-start(bf16[16,8,16,128]{3,1,0,2:T(8,128)(2,1)} %copy.295), calls=%async_computation | async-start | bytes 1048576 | tf_op jit(solution)/shard_map/all_to_all | solution.py:44
  18.9 0.3 convert_reduce_fusion
  19.3 1.0 %fusion.2 = f32[16,128]{1,0:T(8,128)S(1)} fusion(bf16[16,128,512]{2,1,0:T(8,128)(2,1)S(1)} %copy-done.1, f32[16,128]{1,0:T(8,128)S(1)} %broadcast_multiply_fusion), kind=kLoop, calls=%fused_computation.7 | loop fusion | flops 4192256 | bytes 2113536 | tf_op jit(solution)/shard_map/reduce_sum | solution.py:15
  20.3 0.1 copy.299
  20.4 4.4 %fusion.25 = bf16[16,8,16,128]{3,2,1,0:T(8,128)(2,1)} fusion(bf16[16,128,512]{2,1,0:T(8,128)(2,1)S(1)} %copy-done.1, f32[512]{0:T(512)S(1)} %copy-done.7, f32[16,128]{1,0:T(8,128)S(1)} %add_rsqrt_fusion, f32[16,128]{1,0:T(8,128)S(1)} %broadcast_multiply_fusion, bf16[512,512]{1,0:T(8,128)(2,1)} %param.20, bf16[512,16,8]{0,2,1:T(8,128)(2,1)S(1)} %bitcast.140), kind=kOutput, calls=%fused_computation.30 | convolution fusion | flops 1352925184 | bytes 3295232 | tf_op jit(solution)/shard_map/enh,hjc->ecjn/dot_general | solution.py:50
  24.8 4.4 %fusion.62 = (bf16[16,8,1,128]{3,2,1,0:T(2,128)(2,1)S(1)}, bf16[16,8,1,128]{3,2,1,0:T(2,128)(2,1)S(1)}, bf16[16,8,1,128]{3,2,1,0:T(2,128)(2,1)S(1)}, bf16[16,8,1...) fusion(bf16[16,8,16,128]{3,2,1,0:T(8,128)(2,1)} %fusion.25), kind=kLoop, calls=%fused_computation.90 | loop fusion | bytes 1048576 | tf_op jit(solution)/shard_map/split | solution.py:66
  29.2 0.6 constant_dynamic-update-slice_fusion.15
  29.8 0.6 constant_dynamic-update-slice_fusion.14
  30.4 0.6 constant_dynamic-update-slice_fusion.13
  31.1 0.6 constant_dynamic-update-slice_fusion.12
  31.7 0.6 constant_dynamic-update-slice_fusion.11
  32.3 0.6 constant_dynamic-update-slice_fusion.10
  32.9 0.6 constant_dynamic-update-slice_fusion.9
  33.5 0.6 constant_dynamic-update-slice_fusion.8
  34.2 0.6 constant_dynamic-update-slice_fusion.7
  34.8 0.6 constant_dynamic-update-slice_fusion.6
  35.4 0.6 constant_dynamic-update-slice_fusion.5
  36.0 0.6 constant_dynamic-update-slice_fusion.4
  36.6 0.6 constant_dynamic-update-slice_fusion.3
  37.3 0.6 constant_dynamic-update-slice_fusion.2
  37.9 0.6 constant_dynamic-update-slice_fusion.1
  38.5 0.6 constant_dynamic-update-slice_fusion
  39.1 6.0 %all-to-all-start.1 = ((bf16[16,16,8,1,128]{4,2,1,3,0:T(8,128)(2,1)}), bf16[16,16,8,1,128]{4,2,1,3,0:T(8,128)(2,1)S(1)}, u32[]{:S(2)}, u32[]{:S(2)}) async-start(bf16[16,16,8,1,128]{4,2,1,3,0:T(8,128)(2,1)} %constant_dynamic-update-slice_fusion), calls=%async_computation.1 | async-start | bytes 1048576 | tf_op jit(solution)/shard_map/all_to_all | solution.py:66
  45.1 0.6 gather_fusion.1
  45.8 1.1 %fusion.16 = f32[16,128]{1,0:T(8,128)S(1)} fusion(bf16[16,8,16,128]{3,1,0,2:T(8,128)(2,1)} %all-to-all-done), kind=kLoop, calls=%fused_computation.27 | loop fusion | flops 522240 | bytes 532480 | tf_op jit(solution)/shard_map/reduce_sum | solution.py:13
  46.9 1.2 %fusion.31 = f32[16,128]{1,0:T(8,128)S(1)} fusion(f32[16,128]{1,0:T(8,128)S(1)} %broadcast_multiply_fusion.1, bf16[16,8,16,128]{3,1,0,2:T(8,128)(2,1)} %all-to-all-done), kind=kLoop, calls=%fused_computation.32 | loop fusion | flops 1046528 | bytes 540672 | tf_op jit(solution)/shard_map/reduce_sum | solution.py:15
  48.1 11.2 %all-to-all-done.1 = bf16[16,16,8,1,128]{4,2,1,3,0:T(8,128)(2,1)S(1)} async-done(((bf16[16,16,8,1,128]{4,2,1,3,0:T(8,128)(2,1)}), bf16[16,16,8,1,128]{4,2,1,3,0:T(8,128)(2,1)S(1)}, u32[]{:S(2)}, u32[]{:S(2)}) %all-to-all-start.1) | async-done | bytes 524320 | tf_op jit(solution)/shard_map/all_to_all | solution.py:66
  59.4 0.3 copy.301
  59.7 0.4 reshape.155
  60.1 1.4 %copy.302 = bf16[16,8,32,64]{3,1,2,0:T(8,128)(2,1)} copy(bf16[16,8,32,64]{3,2,1,0:T(8,128)(2,1)S(1)} %reshape.155) | data formatting | bytes 1048576 | tf_op jit(solution)/shard_map/reshape | solution.py:70
  61.5 2.2 %gather_fusion.2 = bf16[32,16,8,64]{3,2,1,0:T(8,128)(2,1)S(1)} fusion(bf16[16,8,32,64]{3,1,2,0:T(8,128)(2,1)} %copy.302, s32[1024]{0:T(1024)S(1)} %get-tuple-element.22), kind=kCustom, calls=%fused_computation.2 | custom fusion | bytes 1048704 | tf_op jit(solution)/shard_map/jit(_take)/gather | solution.py:72
  63.7 0.2 select_bitcast_fusion
  63.9 0.4 fusion.15
  64.3 0.7 copy.304
  65.0 1.3 %reshape.156 = bf16[16,8,4096]{2,1,0:T(8,128)(2,1)} reshape(bf16[16,8,32,128]{3,2,1,0:T(8,128)(2,1)S(1)} %copy.304) | data formatting | bytes 2097152 | tf_op jit(solution)/shard_map/reshape | solution.py:75
  66.3 1.8 %convolution_convert_fusion = bf16[16,128,512]{2,1,0:T(8,128)(2,1)S(1)} fusion(f32[128]{0:T(128)S(1)} %copy-done.6, f32[16,128]{1,0:T(8,128)S(1)} %add_rsqrt_fusion.1, f32[16,128]{1,0:T(8,128)S(1)} %broadcast_multiply_fusion.1, bf16[16,8,16,128]{3,1,0,2:T(8,128)(2,1)} %all-to-all-done, bf16[128,512]{1,0:T(8,128)(2,1)S(1)} %copy-done.4), kind=kOutput, calls=%fused_computation.19 | convolution fusion | flops 270794752 | bytes 2769408 | tf_op jit(solution)/shard_map/ecn,ch->enh/dot_general | solution.py:55
  68.1 5.3 %add_convert_fusion = bf16[16,128,512]{2,1,0:T(8,128)(2,1)} fusion(bf16[16,128,512]{2,1,0:T(8,128)(2,1)S(1)} %convolution_convert_fusion, bf16[512,512]{1,0:T(8,128)(2,1)} %param.18, bf16[512,512]{1,0:T(8,128)(2,1)} %param.17), kind=kOutput, calls=%fused_computation.11 | convolution fusion | flops 2155872256 | bytes 5242880 | tf_op jit(solution)/shard_map/enh,hg->eng/dot_general | solution.py:61
  (26 shorter events, 0.1 us)
Async XLA Ops:
  0.6 3.1 %copy-start = (bf16[16,8,4096]{2,1,0:T(8,128)(2,1)S(1)}, bf16[16,8,4096]{2,1,0:T(8,128)(2,1)}, u32[]{:S(2)}) copy-start(bf16[16,8,4096]{2,1,0:T(8,128)(2,1)} %param.11) | copy-start | bytes 3145732
  0.6 4.1 %copy-start.2 = (bf16[32,1,128,64]{2,3,1,0:T(8,128)(2,1)S(1)}, bf16[32,1,128,64]{2,3,1,0:T(8,128)(2,1)}, u32[]{:S(2)}) copy-start(bf16[32,1,128,64]{2,3,1,0:T(8,128)(2,1)} %param.13) | copy-start | bytes 1572868
  6.9 12.0 %copy-start.1 = (bf16[16,128,512]{2,1,0:T(8,128)(2,1)S(1)}, bf16[16,128,512]{2,1,0:T(8,128)(2,1)}, u32[]{:S(2)}) copy-start(bf16[16,128,512]{2,1,0:T(8,128)(2,1)} %param.12) | copy-start | bytes 6291460
  11.4 27.7 %all-to-all-start = ((bf16[16,8,16,128]{3,1,0,2:T(8,128)(2,1)}), bf16[16,8,16,128]{3,1,0,2:T(8,128)(2,1)}, u32[]{:S(2)}, u32[]{:S(2)}) async-start(bf16[16,8,16,128]{3,1,0,2:T(8,128)(2,1)} %copy.295), calls=%async_computation | async-start | bytes 1048576 | tf_op jit(solution)/shard_map/all_to_all | solution.py:44
  18.9 1.4 %copy-start.5 = (bf16[512,128]{1,0:T(8,128)(2,1)S(1)}, bf16[512,128]{1,0:T(8,128)(2,1)}, u32[]{:S(2)}) copy-start(bf16[512,128]{1,0:T(8,128)(2,1)} %param.21) | copy-start | bytes 393220
  18.9 1.5 %copy-start.7 = (f32[512]{0:T(512)S(1)}, f32[512]{0:T(512)}, u32[]{:S(2)}) copy-start(f32[512]{0:T(512)} %param.19) | copy-start | bytes 6148
  24.8 20.3 %copy-start.3 = (bf16[32,1,128,64]{2,3,1,0:T(8,128)(2,1)S(1)}, bf16[32,1,128,64]{2,3,1,0:T(8,128)(2,1)}, u32[]{:S(2)}) copy-start(bf16[32,1,128,64]{2,3,1,0:T(8,128)(2,1)} %param.13) | copy-start | bytes 1572868
  39.1 20.2 %all-to-all-start.1 = ((bf16[16,16,8,1,128]{4,2,1,3,0:T(8,128)(2,1)}), bf16[16,16,8,1,128]{4,2,1,3,0:T(8,128)(2,1)S(1)}, u32[]{:S(2)}, u32[]{:S(2)}) async-start(bf16[16,16,8,1,128]{4,2,1,3,0:T(8,128)(2,1)} %constant_dynamic-update-slice_fusion), calls=%async_computation.1 | async-start | bytes 1048576 | tf_op jit(solution)/shard_map/all_to_all | solution.py:66
  64.3 2.0 %copy-start.4 = (bf16[128,512]{1,0:T(8,128)(2,1)S(1)}, bf16[128,512]{1,0:T(8,128)(2,1)}, u32[]{:S(2)}) copy-start(bf16[128,512]{1,0:T(8,128)(2,1)} %param.16) | copy-start | bytes 393220
  64.3 2.0 %copy-start.6 = (f32[128]{0:T(128)S(1)}, f32[128]{0:T(128)}, u32[]{:S(2)}) copy-start(f32[128]{0:T(128)} %param.15) | copy-start | bytes 1540
